TPU v7x, 32 devices: a whole 2x2x4 slice. The times are simulated.
32 devices in a mesh: fsdp: 8 (over y, x, core), seq: 4 (over z).
Axes of the slice: x: 2, y: 2, z: 4, core: 2. Of those that a mesh axis runs over, the one named last changes fastest.
Arguments:
- tokens: bfloat16 [8, 2048, 4096], P('fsdp', 'seq'), may hold values from -72 to 72
- norm_gain: float32 [4096], replicated, may hold values from 0.1 to 1.9
- lru_proj: bfloat16 [4096, 2048], P(('fsdp', 'seq')), may hold values from -0.09375 to 0.09375
- gelu_proj: bfloat16 [4096, 2048], P(('fsdp', 'seq')), may hold values from -0.09375 to 0.09375
- conv_weight: float32 [4, 2048], replicated, may hold values from -3 to 3
- conv_bias: float32 [2048], replicated, may hold values from -3 to 3
- gate_weights: bfloat16 [2048, 512], P('seq'), may hold values from -0.375 to 0.375
- gate_bias: float32 [2, 2048], replicated, may hold values from -4 to 4
- decay_param: float32 [2048], replicated, may hold values from -13 to -2
Outputs:
- recurrent_out: bfloat16 [8, 2048, 2048], P('fsdp', 'seq')
All inputs are finite; a program needn't handle non-finite values.
Results may differ from a plain program's by a relative error of at most 0.0051.
Values may be sent and summed in bfloat16 or wider, within the bound.
A program may use at most 128 MiB of HBM per device.

v0:
```python
import jax
import jax.numpy as jnp
from jax import lax
from jax.sharding import PartitionSpec as P


def from_behind(x, axis, by):
    devices = lax.axis_size(axis)
    pairs = [(i, i + by) for i in range(devices) if 0 <= i + by < devices]
    return lax.ppermute(x, axis, pairs)


def block_scan(decay, driven):
    seq_count, tok_rows, inner = decay.shape
    block_rows = tok_rows
    for candidate in (64, 32, 16, 8):
        block_rows = candidate
        break
    block_count = tok_rows // block_rows
    decay_blocks = decay.reshape(seq_count, block_count, block_rows, inner)
    driven_blocks = driven.reshape(seq_count, block_count, block_rows, inner)
    running_decay = decay_blocks[:, :, 0]
    running_state = driven_blocks[:, :, 0]
    decay_list = [running_decay]
    state_list = [running_state]
    for offset in range(1, block_rows):
        decay_now = decay_blocks[:, :, offset]
        running_decay = running_decay * decay_now
        running_state = decay_now * running_state + driven_blocks[:, :, offset]
        decay_list.append(running_decay)
        state_list.append(running_state)
    within_decay = jnp.stack(decay_list, axis=2)
    within_state = jnp.stack(state_list, axis=2)
    carry_state = jnp.zeros((seq_count, inner), jnp.float32)
    carry_decay = jnp.ones((seq_count, inner), jnp.float32)
    start_list = []
    prefix_list = []
    for block_index in range(block_count):
        start_list.append(carry_state)
        prefix_list.append(carry_decay)
        carry_state = running_decay[:, block_index] * carry_state + running_state[:, block_index]
        carry_decay = carry_decay * running_decay[:, block_index]
    block_start = jnp.stack(start_list, axis=1)
    block_prefix = jnp.stack(prefix_list, axis=1)
    cumulative = (within_decay * block_prefix[:, :, None, :]).reshape(seq_count, tok_rows, inner)
    local_state = (within_state + within_decay * block_start[:, :, None, :]).reshape(
        seq_count, tok_rows, inner
    )
    return (cumulative, local_state, carry_decay, carry_state)


def shards(
    tokens,
    norm_gain,
    lru_proj,
    gelu_proj,
    conv_weight,
    conv_bias,
    gate_weights,
    gate_bias,
    decay_param,
):
    seq_count, tok_rows, width = tokens.shape
    inner = lru_proj.shape[1]
    block_width = gate_weights.shape[1] // 2
    head_count = inner // block_width
    taps = conv_weight.shape[0]
    flat_tokens = tokens.reshape(seq_count * tok_rows, width).astype(jnp.float32)
    mean_square = jnp.mean(flat_tokens * flat_tokens, axis=-1, keepdims=True)
    normed = (flat_tokens * lax.rsqrt(mean_square + 1e-06) * norm_gain).astype(jnp.bfloat16)
    branch = jnp.dot(
        normed,
        lax.all_gather(lru_proj, ("fsdp", "seq"), axis=0, tiled=True),
        preferred_element_type=jnp.float32,
    )
    gelu_in = jnp.dot(
        normed,
        lax.all_gather(gelu_proj, ("fsdp", "seq"), axis=0, tiled=True),
        preferred_element_type=jnp.float32,
    )
    recurrent_in = branch.astype(jnp.bfloat16).reshape(seq_count, tok_rows, inner)
    last_rows = recurrent_in[:, tok_rows - (taps - 1) :, :]
    before = from_behind(last_rows, "seq", 1)
    padded = jnp.concatenate([before, recurrent_in], axis=1)
    conv_sum = jnp.zeros((seq_count, tok_rows, inner), jnp.float32) + conv_bias
    for tap_index in range(taps):
        begin = taps - 1 - tap_index
        conv_sum = conv_sum + conv_weight[tap_index] * padded[
            :, begin : begin + tok_rows, :
        ].astype(jnp.float32)
    conv_out = conv_sum.astype(jnp.bfloat16)
    gate_table = lax.all_gather(gate_weights, "seq", axis=0, tiled=True)
    gate_all = jnp.einsum(
        "nhi,hij->nhj",
        conv_out.reshape(-1, head_count, block_width),
        gate_table.reshape(head_count, block_width, 2 * block_width),
        preferred_element_type=jnp.float32,
    )
    input_gate = jax.nn.sigmoid(
        gate_all[:, :, :block_width].reshape(seq_count, tok_rows, inner) + gate_bias[0]
    )
    recur_gate = jax.nn.sigmoid(
        gate_all[:, :, block_width:].reshape(seq_count, tok_rows, inner) + gate_bias[1]
    )
    log_decay = -8.0 * jax.nn.softplus(decay_param) * recur_gate
    decay = jnp.exp(log_decay)
    driven = jnp.sqrt(-jnp.expm1(2.0 * log_decay)) * input_gate * conv_out.astype(jnp.float32)
    cumulative, local_state, total_decay, end_state = block_scan(decay, driven)
    start_state = jnp.zeros_like(end_state)
    for hop_index in range(lax.axis_size("seq") - 1):
        start_state = from_behind(total_decay * start_state + end_state, "seq", 1)
    state = local_state + cumulative * start_state[:, None, :]
    gelu_part = jax.nn.gelu(gelu_in.reshape(seq_count, tok_rows, inner), approximate=True)
    return (state * gelu_part).astype(jnp.bfloat16)


def solution(mesh):
    placed = (
        P("fsdp", "seq", None),
        P(),
        P(("fsdp", "seq"), None),
        P(("fsdp", "seq"), None),
        P(),
        P(),
        P("seq", None),
        P(),
        P(),
    )
    return jax.shard_map(
        shards, mesh=mesh, in_specs=placed, out_specs=P("fsdp", "seq", None), check_vma=False
    )
```

profile of v0, /device:TPU:0, one launch (start us, length us, event | category | flops | bytes accessed | tf_op | source)
XLA Modules:
  0.0 346.6 jit_solution(16968353154089709732)
XLA Ops:
  8.8 3.1 fusion
  12.0 115.5 %all-gather.4.cloned.1.call-done = bf16[4096,2048]{1,0:T(8,128)(2,1)} async-done(((bf16[128,2048]{1,0:T(8,128)(2,1)}), bf16[4096,2048]{1,0:T(8,128)(2,1)}) %all-gather.4.cloned.1.call-update) | async-done | bytes 16777232 | tf_op jit(solution)/shard_map/all_gather | solution.py:73
  127.5 13.7 %convolution_convert_fusion = bf16[512,2048]{1,0:T(8,128)(2,1)S(1)} fusion(bf16[4096,2048]{1,0:T(8,128)(2,1)} %all-gather.4.cloned.1.call-done, bf16[1,512,4096]{2,1,0:T(8,128)(2,1)} %param.9, f32[4096]{0:T(1024)S(1)} %copy-done.13, f32[512]{0:T(512)S(1)} %add_rsqrt_fusion), kind=kOutput, calls=%fused_computation.27 | convolution fusion | flops 8599371776 | bytes 23087104 | tf_op jit(solution)/shard_map/dot_general | solution.py:71
  141.2 3.0 collective-permute-start
  145.4 2.3 fusion.16
  147.8 2.0 copy.406
  149.8 23.2 %all-gather.6.cloned.1.call-done = bf16[2048,512]{1,0:T(8,128)(2,1)} async-done(((bf16[512,512]{1,0:T(8,128)(2,1)}), bf16[2048,512]{1,0:T(8,128)(2,1)}) %all-gather.6.cloned.1.call-update) | async-done | bytes 2097168 | tf_op jit(solution)/shard_map/all_gather | solution.py:92
  172.9 3.6 %convolution_bitcast_fusion = f32[512,8,512]{0,2,1:T(8,128)S(1)} fusion(bf16[8,256,512]{2,1,0:T(8,128)(2,1)} %bitcast.2080, bf16[512,8,256]{2,1,0:T(8,128)(2,1)} %bitcast.2079), kind=kOutput, calls=%fused_computation.26 | convolution fusion | flops 1073741824 | bytes 12582912 | tf_op jit(solution)/shard_map/nhi,hij->nhj/dot_general | solution.py:93
  176.5 4.3 %fusion.147 = (f32[512,8,256]{0,2,1:T(8,128)}, f32[512,8,256]{0,2,1:T(8,128)}) fusion(f32[512,8,512]{0,2,1:T(8,128)S(1)} %convolution_bitcast_fusion), kind=kLoop, calls=%fused_computation.551 | loop fusion | bytes 16777216 | tf_op jit(solution)/shard_map/slice | solution.py:103
  180.8 5.6 %copy.83 = f32[512,8,256]{2,1,0:T(8,128)} copy(f32[512,8,256]{0,2,1:T(8,128)} %get-tuple-element.111) | data formatting | bytes 8388608 | tf_op jit(solution)/shard_map/slice | solution.py:103
  186.4 5.4 %copy.275 = f32[1,512,2048]{2,1,0:T(8,128)} copy(f32[1,512,2048]{1,2,0:T(8,128)} %bitcast.2074) | data formatting | bytes 8388608 | tf_op jit(solution)/shard_map/reshape | solution.py:103
  191.8 5.4 %copy.276 = f32[1,512,2048]{2,1,0:T(8,128)} copy(f32[1,512,2048]{1,2,0:T(8,128)} %bitcast.2076) | data formatting | bytes 8388608 | tf_op jit(solution)/shard_map/reshape | solution.py:100
  197.2 4.9 %reshape.9618 = f32[1,8,64,2048]{3,2,1,0:T(8,128)} reshape(f32[512,8,256]{2,1,0:T(8,128)} %copy.83) | data formatting | bytes 8388608 | tf_op jit(solution)/shard_map/reshape | solution.py:103
  202.1 4.0 %multiply_exponential_fusion = f32[1,8,64,2048]{3,2,1,0:T(8,128)S(1)} fusion(f32[1,8,64,2048]{3,2,1,0:T(8,128)} %reshape.9618, f32[2048]{0:T(1024)S(1)} %bitcast.2111, f32[2048]{0:T(1024)S(1)} %fusion.94), kind=kLoop, calls=%fused_computation.24 | loop fusion | flops 5242880 | bytes 8404992 | tf_op jit(solution)/shard_map/exp | solution.py:106
  206.1 3.0 fusion.85
  209.8 4.3 %convert_multiply_fusion.2 = f32[1,512,2048]{2,1,0:T(8,128)S(1)} fusion(bf16[1,512,2048]{2,1,0:T(8,128)(2,1)S(1)} %fusion.16, f32[1,512,2048]{2,1,0:T(8,128)S(1)} %copy-done.4, f32[1,512,2048]{2,1,0:T(8,128)S(1)} %copy-done.3, f32[2048]{0:T(1024)S(1)} %bitcast.2115, f32[2048]{0:T(1024)S(1)} %bitcast.2112, f32[2048]{0:T(1024)S(1)} %fusion.94), kind=kLoop, calls=%fused_computation.25 | loop fusion | flops 14680064 | bytes 14704640 | tf_op jit(solution)/shard_map/mul | solution.py:107
  214.1 6.4 %bitcast_add_fusion.2 = (f32[1,8,2048]{2,0,1:T(1,128)S(1)}, f32[1,8,1,2048]{3,0,2,1:T(1,128)S(1)}, f32[1,8,1,2048]{3,0,2,1:T(1,128)S(1)}, f32[1,8,1,2048]{3,0,2,...) fusion(f32[1,8,64,2048]{3,2,1,0:T(8,128)S(1)} %bitcast.2014, ...), kind=kLoop, calls=%fused_computation.140 | loop fusion | flops 2064384 | bytes 8716288 | tf_op jit(solution)/shard_map/add | solution.py:29
  220.7 2.1 collective-permute-start.1
  227.0 1.3 constant_dynamic-update-slice_fusion.34
  228.3 1.8 constant_dynamic-update-slice_fusion.33
  231.5 1.7 constant_dynamic-update-slice_fusion.31
  234.6 1.8 constant_dynamic-update-slice_fusion.29
  236.4 1.7 constant_dynamic-update-slice_fusion.28
  238.0 2.0 constant_dynamic-update-slice_fusion.27
  241.4 1.9 constant_dynamic-update-slice_fusion.25
  244.7 1.7 constant_dynamic-update-slice_fusion.23
  247.8 2.0 constant_dynamic-update-slice_fusion.21
  251.1 2.0 constant_dynamic-update-slice_fusion.19
  254.5 2.0 constant_dynamic-update-slice_fusion.17
  257.8 1.7 constant_dynamic-update-slice_fusion.15
  260.9 1.9 constant_dynamic-update-slice_fusion.13
  262.8 1.4 constant_dynamic-update-slice_fusion.12
  264.1 1.9 constant_dynamic-update-slice_fusion.11
  267.4 1.9 constant_dynamic-update-slice_fusion.9
  269.3 1.6 constant_dynamic-update-slice_fusion.8
  270.8 1.7 constant_dynamic-update-slice_fusion.7
  273.9 1.8 constant_dynamic-update-slice_fusion.5
  275.7 1.4 constant_dynamic-update-slice_fusion.4
  277.1 1.8 constant_dynamic-update-slice_fusion.3
  278.8 3.0 slice_multiply_fusion
  281.8 2.3 fusion.111
  284.2 1.5 constant_dynamic-update-slice_fusion.1
  288.4 1.4 fusion.121
  289.8 3.4 collective-permute-start.2
  294.6 4.8 %collective-permute-start.3 = (f32[1,2048]{1,0:T(1,128)S(1)}, f32[1,2048]{1,0:T(1,128)}, u32[]{:S(2)}, u32[]{:S(2)}) collective-permute-start(f32[1,2048]{1,0:T(1,128)S(1)} %multiply_add_fusion), channel_id=1, source_target_pairs={{0,1},{1,2},{2,3},{4,5},{5,6},{6,7},{8,9},{9,10},{10,11},{12,13},{... | collective-permute-start | bytes 24584 | tf_op jit(solution)/shard_map/ppermute | solution.py:10
  301.4 3.9 %copy.277 = f32[1,8,64,2048]{3,2,0,1:T(8,128)} copy(f32[1,8,64,2048]{3,0,2,1:T(1,128)S(1)} %constant_dynamic-update-slice_fusion) | data formatting | bytes 8388608
  305.3 15.1 %stack.14 = f32[1,8,64,2048]{3,2,1,0:T(8,128)} concatenate(f32[1,8,1,2048]{3,2,1,0:T(1,128)} %slice.766, f32[1,8,1,2048]{3,2,1,0:T(1,128)S(1)} %get-tuple-element.139, f32[1,8,1,2048]{3,2,1,0:T(1,128)S(1)} %bitcast.2084, f32[1,8,1,2048]{3,2,1,0:T(1,128)S(1)} %get-tuple-element.137, f32[1,8,1,2048]{3,2,1,0:T(1,128)S(1)} %bitcast.2083, f32[1,8,1,2048]{3,2,1,0:T(1,128)S(1)} %get-tuple-element.135, ...), dimensions={2} | concatenate | bytes 8388608 | tf_op jit(solution)/shard_map/stack | solution.py:32
  320.5 19.4 %fusion.11 = bf16[512,2048]{1,0:T(8,128)(2,1)} fusion(f32[1,8,64,2048]{3,2,0,1:T(8,128)} %copy.277, f32[1,8,64,2048]{3,2,1,0:T(8,128)} %stack.14, f32[2048]{0:T(1024)} %bitcast.211, f32[8,2048]{1,0:T(8,128)} %bitcast.2113, f32[8,2048]{1,0:T(8,128)} %bitcast.2114, bf16[4096,2048]{1,0:T(8,128)(2,1)} %all-gather.8.cloned.1.call-done, ...), kind=kOutput, calls=%fused_computation.14 | convolution fusion | flops 8614051840 | bytes 31614976 | tf_op jit(solution)/shard_map/dot_general | solution.py:76
  (107 shorter events, 29.3 us)
Async XLA Ops:
  6.5 5.3 %copy-start.9 = (f32[4,2048]{1,0:T(4,128)S(1)}, f32[4,2048]{1,0:T(4,128)}, u32[]{:S(2)}) copy-start(f32[4,2048]{1,0:T(4,128)} %param.13) | copy-start | bytes 98308
  6.5 5.4 %copy-start.10 = (f32[2,2048]{1,0:T(2,128)S(1)}, f32[2,2048]{1,0:T(2,128)}, u32[]{:S(2)}) copy-start(f32[2,2048]{1,0:T(2,128)} %param.16) | copy-start | bytes 49156
  6.5 5.4 %copy-start.12 = (f32[2048]{0:T(1024)S(1)}, f32[2048]{0:T(1024)}, u32[]{:S(2)}) copy-start(f32[2048]{0:T(1024)} %param.17) | copy-start | bytes 24580
  6.5 120.9 %copy-start.13 = (f32[4096]{0:T(1024)S(1)}, f32[4096]{0:T(1024)}, u32[]{:S(2)}) copy-start(f32[4096]{0:T(1024)} %param.10) | copy-start | bytes 49156
  6.5 120.9 %all-gather.4.cloned.1.call-start = ((), (), s32[]{:S(2)}) async-start(), calls=%async_computation | async-start | bytes 17301504 | tf_op jit(solution)/shard_map/all_gather | solution.py:73
  7.3 165.7 %all-gather.6.cloned.1.call-start = ((), (), s32[]{:S(2)}) async-start(), calls=%async_computation.1 | async-start | bytes 2621440 | tf_op jit(solution)/shard_map/all_gather | solution.py:92
  8.0 312.4 %all-gather.8.cloned.1.call-start = ((), (), s32[]{:S(2)}) async-start(), calls=%async_computation.2 | async-start | bytes 17301504 | tf_op jit(solution)/shard_map/all_gather | solution.py:78
  12.0 133.5 %copy-start.11 = (f32[2048]{0:T(1024)S(1)}, f32[2048]{0:T(1024)}, u32[]{:S(2)}) copy-start(f32[2048]{0:T(1024)} %param.14) | copy-start | bytes 24580
  141.2 4.3 %collective-permute-start = (bf16[1,3,2048]{2,1,0:T(4,128)(2,1)S(1)}, bf16[1,3,2048]{2,1,0:T(4,128)(2,1)S(1)}, u32[]{:S(2)}, u32[]{:S(2)}) collective-permute-start(bf16[1,3,2048]{2,1,0:T(4,128)(2,1)S(1)} %slice.632), channel_id=1, source_target_pairs={{0,1},{1,2},{2,3},{4,5},{5,6},{6,7},{8,9},{9,10},{10,11},{12,13},{... | collective-permute-start | bytes 36872 | tf_op jit(solution)/shard_map/ppermute | solution.py:10
  202.1 7.0 %copy-start.4 = (f32[1,512,2048]{2,1,0:T(8,128)S(1)}, f32[1,512,2048]{2,1,0:T(8,128)}, u32[]{:S(2)}) copy-start(f32[1,512,2048]{2,1,0:T(8,128)} %copy.276) | copy-start | bytes 12582916
  206.1 20.7 %copy-start = (f32[1,8,64,2048]{3,2,1,0:T(8,128)}, f32[1,8,64,2048]{3,2,1,0:T(8,128)S(1)}, u32[]{:S(2)}) copy-start(f32[1,8,64,2048]{3,2,1,0:T(8,128)S(1)} %multiply_exponential_fusion) | copy-start | bytes 12582916
  206.1 3.7 %copy-start.3 = (f32[1,512,2048]{2,1,0:T(8,128)S(1)}, f32[1,512,2048]{2,1,0:T(8,128)}, u32[]{:S(2)}) copy-start(f32[1,512,2048]{2,1,0:T(8,128)} %copy.275) | copy-start | bytes 12582916
  214.1 12.7 %copy-start.2 = (f32[1,512,2048]{2,1,0:T(8,128)}, f32[1,512,2048]{2,1,0:T(8,128)S(1)}, u32[]{:S(2)}) copy-start(f32[1,512,2048]{2,1,0:T(8,128)S(1)} %convert_multiply_fusion.2) | copy-start | bytes 12582916
  220.7 69.1 %collective-permute-start.1 = (f32[1,2048]{1,0:T(1,128)S(1)}, f32[1,2048]{1,0:T(1,128)S(1)}, u32[]{:S(2)}, u32[]{:S(2)}) collective-permute-start(f32[1,2048]{1,0:T(1,128)S(1)} %get-tuple-element.15), channel_id=1, source_target_pairs={{0,1},{1,2},{2,3},{4,5},{5,6},{6,7},{8,9},{9,10},{10,11},{12,13},{... | collective-permute-start | bytes 24584 | tf_op jit(solution)/shard_map/ppermute | solution.py:10
  223.4 9.8 %copy-start.7 = (f32[1,8,2048]{2,0,1:T(1,128)}, f32[1,8,2048]{2,0,1:T(1,128)S(1)}, u32[]{:S(2)}) copy-start(f32[1,8,2048]{2,0,1:T(1,128)S(1)} %get-tuple-element.145) | copy-start | bytes 196612
  223.4 9.8 %copy-start.5 = (f32[1,8,2048]{2,0,1:T(1,128)}, f32[1,8,2048]{2,0,1:T(1,128)S(1)}, u32[]{:S(2)}) copy-start(f32[1,8,2048]{2,0,1:T(1,128)S(1)} %constant_dynamic-update-slice_fusion.75) | copy-start | bytes 196612
  241.4 37.5 %copy-start.1 = (f32[1,8,64,2048]{3,2,1,0:T(8,128)S(1)}, f32[1,8,64,2048]{3,2,1,0:T(8,128)}, u32[]{:S(2)}) copy-start(f32[1,8,64,2048]{3,2,1,0:T(8,128)} %copy-done) | copy-start | bytes 12582916
  281.8 7.9 %copy-start.6 = (f32[1,8,2048]{2,0,1:T(1,128)S(1)}, f32[1,8,2048]{2,0,1:T(1,128)}, u32[]{:S(2)}) copy-start(f32[1,8,2048]{2,0,1:T(1,128)} %copy-done.5) | copy-start | bytes 196612
  281.8 18.9 %copy-start.8 = (f32[1,8,2048]{2,0,1:T(1,128)S(1)}, f32[1,8,2048]{2,0,1:T(1,128)}, u32[]{:S(2)}) copy-start(f32[1,8,2048]{2,0,1:T(1,128)} %copy-done.7) | copy-start | bytes 196612
  289.8 4.8 %collective-permute-start.2 = (f32[1,2048]{1,0:T(1,128)S(1)}, f32[1,2048]{1,0:T(1,128)S(1)}, u32[]{:S(2)}, u32[]{:S(2)}) collective-permute-start(f32[1,2048]{1,0:T(1,128)S(1)} %multiply_add_fusion.1), channel_id=1, source_target_pairs={{0,1},{1,2},{2,3},{4,5},{5,6},{6,7},{8,9},{9,10},{10,11},{12,13},{... | collective-permute-start | bytes 24584 | tf_op jit(solution)/shard_map/ppermute | solution.py:10
  294.6 25.9 %collective-permute-start.3 = (f32[1,2048]{1,0:T(1,128)S(1)}, f32[1,2048]{1,0:T(1,128)}, u32[]{:S(2)}, u32[]{:S(2)}) collective-permute-start(f32[1,2048]{1,0:T(1,128)S(1)} %multiply_add_fusion), channel_id=1, source_target_pairs={{0,1},{1,2},{2,3},{4,5},{5,6},{6,7},{8,9},{9,10},{10,11},{12,13},{... | collective-permute-start | bytes 24584 | tf_op jit(solution)/shard_map/ppermute | solution.py:10
Sparse Core Ops, SparseCore 0:
  10.3 117.0 all-gather.3
  129.0 43.8 all-gather.5
  175.9 113.5 all-gather.7
where the time goes:
time: 352 us; the launch traced here: 347 us
  waiting for transfers between devices  143 us (41%)
  other arithmetic  90 us (26%)
  local copies, waits for them, and re-layouts  49.5 us (14%)
  matrix products  36.6 us (10%)
  between operations  13.8 us (4%)
  starting transfers between devices  13.5 us (4%)
    all_gather x1, waiting for transfers between devices, shards(): lax.all_gather(lru_proj, ('fsdp', 'seq'), axis=0, tiled=True)  115 us
    unnamed x66, other arithmetic  57.4 us
    all_gather x1, waiting for transfers between devices, shards(): gate_table = lax.all_gather(gate_weights, 'seq', axis=0, tiled=True)  23.2 us
    dot_general x1, matrix products, shards(): jnp.dot(normed, lax.all_gather(gelu_proj, ('fsdp', 'seq'), axis=0, tiled=...  19.4 us
    another operation x1, local copies, waits for them, and re-layouts, block_scan(): within_decay = jnp.stack(decay_list, axis=2)  15.1 us
    dot_general x1, matrix products, shards(): jnp.dot(normed, lax.all_gather(lru_proj, ('fsdp', 'seq'), axis=0, tiled=T...  13.7 us
    ppermute x4, starting transfers between devices, from_behind(): return lax.ppermute(x, axis, pairs)  13.3 us
    mul x6, other arithmetic, block_scan(): running_decay = running_decay * decay_now  11.1 us
  transfers between devices with their start and end apart: 7, of which 4 were waited for; matrix products, arithmetic and copies ran while one was open for 45% of the time, Pallas kernels for 0%

commit v1 on v0

v1 whole, which is shorter than its diff:
```python
import functools

import jax
import jax.numpy as jnp
from jax import lax
from jax.experimental import pallas as pl
from jax.experimental.pallas import tpu as pltpu
from jax.sharding import PartitionSpec as P

MESH = pl.DeviceIdType.MESH
LANES = 128
VMEM_BYTES = 66_000_000


def normalise(tokens_ref, gain_ref, normed_ref):
    rows = 32

    def body(i, _):
        at = pl.ds(pl.multiple_of(i * rows, rows), rows)
        values = tokens_ref[at, :].astype(jnp.float32)
        mean_square = jnp.mean(values * values, axis=-1, keepdims=True)
        normed_ref[at, :] = (values * lax.rsqrt(mean_square + 1e-06) * gain_ref[...]).astype(jnp.bfloat16)
        return 0

    lax.fori_loop(0, tokens_ref.shape[0] // rows, body, 0)


def gather_kernel(
    nz,
    tokens_ref, gain_ref, lru_ref, gelu_ref, gate_ref,
    rec_ref, act_ref, table_ref,
    w_ref, normed_ref, own_sem, send_sem, core_send, gate_send,
    z_recv, gate_recv, x_recv, y_recv, a_recv, b_recv, core_recv,
):
    f = lax.axis_index("fsdp")
    z = lax.axis_index("seq")
    c, x, y = f % 2, (f // 2) % 2, f // 4
    fx, fy, fc = f + 2 - 4 * x, f + 4 - 8 * y, f + 1 - 2 * c
    fd = fx + 4 - 8 * y
    shard = lru_ref.shape[0]
    line = shard * nz
    half = line // 2
    chunks = w_ref.shape[0]
    split = chunks // 2
    gate_rows = gate_ref.shape[0]
    piece = gate_rows // split

    def remote(src, send, recv, device):
        return pltpu.make_async_remote_copy(
            src_ref=src, dst_ref=src, send_sem=send, recv_sem=recv,
            device_id=device, device_id_type=MESH,
        )

    own = pl.ds(pl.multiple_of((f * nz + z) * shard, shard), shard)
    for t in range(chunks):
        src = lru_ref if t < split else gelu_ref
        cols = pl.ds((t % split) * LANES, LANES)
        pltpu.make_async_copy(src.at[:, cols], w_ref.at[t, own], own_sem.at[0]).start()
    own_gate = pl.ds(pl.multiple_of(z * gate_rows, gate_rows), gate_rows)
    gate_copy = pltpu.make_async_copy(gate_ref, table_ref.at[own_gate], own_sem.at[1])
    gate_copy.start()

    barrier = pltpu.get_barrier_semaphore()
    for device in ((fx, z), (fy, z), (fc, z)):
        pl.semaphore_signal(barrier, inc=1, device_id=device, device_id_type=MESH)

    @pl.when(z > 0)
    def _():
        pl.semaphore_signal(barrier, inc=1, device_id=(f, z - 1), device_id_type=MESH)

    @pl.when(z < nz - 1)
    def _():
        pl.semaphore_signal(barrier, inc=1, device_id=(f, z + 1), device_id_type=MESH)

    for k in range(nz):
        @pl.when(z == k)
        def _():
            pl.semaphore_wait(barrier, 3 + int(k > 0) + int(k < nz - 1))

    pltpu.make_async_copy(w_ref.at[:, own], w_ref.at[:, own], own_sem.at[0]).wait()
    gate_copy.wait()

    def shard_of(t, source):
        at = pl.ds(pl.multiple_of((f * nz + source) * shard, shard), shard)
        return w_ref.at[t, at]

    def gate_of(t, source):
        at = pl.ds(pl.multiple_of(source * gate_rows + t * piece, piece), piece)
        return table_ref.at[at]

    def pass_on(t, source, target):
        remote(shard_of(t, source), send_sem.at[t], z_recv.at[t, source], (f, target)).start()

        @pl.when(t < split)
        def _():
            remote(gate_of(t, source), gate_send.at[t], gate_recv.at[t, source], (f, target)).start()

    def arrived(t, source):
        remote(shard_of(t, source), send_sem.at[t], z_recv.at[t, source], (f, z)).wait_recv()

        @pl.when(t < split)
        def _():
            remote(gate_of(t, source), gate_send.at[t], gate_recv.at[t, source], (f, z)).wait_recv()

    def z_first(t):
        @pl.when(z > 0)
        def _():
            pass_on(t, z, z - 1)

        @pl.when(z < nz - 1)
        def _():
            pass_on(t, z, z + 1)

    def z_hop(t, distance):
        @pl.when(z >= distance)
        def _():
            arrived(t, z - distance)

            @pl.when(z < nz - 1)
            def _():
                pass_on(t, z - distance, z + 1)

        @pl.when(z + distance < nz)
        def _():
            arrived(t, z + distance)

            @pl.when(z > 0)
            def _():
                pass_on(t, z + distance, z - 1)

    def rows_of(owner, t, start, size):
        return w_ref.at[t, pl.ds(pl.multiple_of(owner * line + start, shard), size)]

    def to_core(t, owner, start, size):
        remote(rows_of(owner, t, start, size), core_send.at[t], core_recv.at[t], (fc, z)).start()

    def line_done(t):
        mine = rows_of(f, t, 0, line)
        remote(mine, send_sem.at[t], x_recv.at[t], (fx, z)).start()
        remote(mine, send_sem.at[t], y_recv.at[t], (fy, z)).start()
        to_core(t, f, 0, line)

    def sides_done(t):
        from_x = rows_of(fx, t, 0, line)
        remote(from_x, send_sem.at[t], x_recv.at[t], (fx, z)).wait_recv()
        remote(rows_of(fx, t, 0, half), send_sem.at[t], a_recv.at[t], (fy, z)).start()
        to_core(t, fx, 0, line)
        from_y = rows_of(fy, t, 0, line)
        remote(from_y, send_sem.at[t], y_recv.at[t], (fy, z)).wait_recv()
        remote(rows_of(fy, t, half, half), send_sem.at[t], b_recv.at[t], (fx, z)).start()
        to_core(t, fy, 0, line)

    def corner_done(t):
        remote(rows_of(fd, t, 0, half), send_sem.at[t], a_recv.at[t], (fy, z)).wait_recv()
        to_core(t, fd, 0, half)
        remote(rows_of(fd, t, half, half), send_sem.at[t], b_recv.at[t], (fx, z)).wait_recv()
        to_core(t, fd, half, half)

    def multiply(t):
        whole = w_ref.at[t, pl.ds(0, 4 * line)]
        pltpu.make_async_copy(whole, whole, core_recv.at[t]).wait()
        blocks = normed_ref.shape[0] // 256
        column = pl.ds(pl.multiple_of((t % split) * LANES, LANES), LANES)

        def body(i, _):
            at = pl.ds(pl.multiple_of(i * 256, 256), 256)
            product = jnp.dot(normed_ref[at, :], w_ref[t], preferred_element_type=jnp.float32)

            @pl.when(t < split)
            def _():
                rec_ref[at, column] = product.astype(jnp.bfloat16)

            @pl.when(t >= split)
            def _():
                act_ref[at, column] = product

            return 0

        lax.fori_loop(0, blocks, body, 0)

    stages = [z_first]
    for distance in range(1, nz):
        stages.append(functools.partial(z_hop, distance=distance))
    stages += [line_done, sides_done, corner_done, multiply]
    lags = list(range(nz)) + [nz - 1, nz, nz + 1, nz + 2]

    def step(t, _):
        for stage, lag in zip(stages, lags):
            @pl.when((t >= lag) & (t < chunks + lag))
            def _():
                stage(t - lag)

        @pl.when(t == 0)
        def _():
            normalise(tokens_ref, gain_ref, normed_ref)

        return 0

    lax.fori_loop(0, chunks + lags[-1], step, 0)

    def drain(t, _):
        for k in range(nz):
            shards_sent = (k + 1 if k < nz - 1 else 0) + (nz - k if k > 0 else 0)

            @pl.when(z == k)
            def _():
                sent = w_ref.at[t, pl.ds(0, shards_sent * shard + 3 * line)]
                pltpu.make_async_copy(sent, sent, send_sem.at[t]).wait()

                @pl.when(t < split)
                def _():
                    sent_gate = table_ref.at[pl.ds(0, shards_sent * piece)]
                    pltpu.make_async_copy(sent_gate, sent_gate, gate_send.at[t]).wait()

        whole = w_ref.at[t, pl.ds(0, 4 * line)]
        pltpu.make_async_copy(whole, whole, core_send.at[t]).wait()
        return 0

    lax.fori_loop(0, chunks, drain, 0)


def gathered_products(nz, tokens, norm_gain, lru_proj, gelu_proj, gate_weights):
    rows, width = tokens.shape
    inner = lru_proj.shape[1]
    chunks = 2 * inner // LANES
    vmem = pl.BlockSpec(memory_space=pltpu.VMEM)
    any_ = pl.BlockSpec(memory_space=pl.ANY)
    dma = pltpu.SemaphoreType.DMA
    return pl.pallas_call(
        functools.partial(gather_kernel, nz),
        out_shape=(
            jax.ShapeDtypeStruct((rows, inner), jnp.bfloat16),
            jax.ShapeDtypeStruct((rows, inner), jnp.float32),
            jax.ShapeDtypeStruct((gate_weights.shape[0] * nz, gate_weights.shape[1]), jnp.bfloat16),
        ),
        in_specs=[vmem, vmem, any_, any_, any_],
        out_specs=(vmem, vmem, vmem),
        scratch_shapes=[
            pltpu.VMEM((chunks, width, LANES), jnp.bfloat16),
            pltpu.VMEM((rows, width), jnp.bfloat16),
            dma((2,)), dma((chunks,)), dma((chunks,)), dma((chunks // 2,)),
            dma((chunks, nz)), dma((chunks // 2, nz)),
            dma((chunks,)), dma((chunks,)), dma((chunks,)), dma((chunks,)), dma((chunks,)),
        ],
        compiler_params=pltpu.CompilerParams(
            collective_id=0, has_side_effects=True, vmem_limit_bytes=VMEM_BYTES
        ),
    )(tokens, norm_gain.reshape(1, width), lru_proj, gelu_proj, gate_weights)


def scan_kernel(
    rec_ref, before_ref, weight_ref, bias_ref, table_ref, gate_bias_ref, decay_ref,
    state_ref, cumulative_ref, end_ref, padded_ref, a_ref, b_ref,
):
    rows, channels = rec_ref.shape
    taps = weight_ref.shape[0]
    lead = before_ref.shape[0]
    padded_ref[pl.ds(0, lead), :] = before_ref[...].astype(jnp.float32)
    padded_ref[pl.ds(lead, rows), :] = rec_ref[...].astype(jnp.float32)
    conv_sum = jnp.zeros((rows, channels), jnp.float32) + bias_ref[...]
    for tap in range(taps):
        conv_sum = conv_sum + weight_ref[tap : tap + 1, :] * padded_ref[pl.ds(lead - tap, rows), :]
    conv_out = conv_sum.astype(jnp.bfloat16)
    gates = jnp.dot(conv_out, table_ref[...], preferred_element_type=jnp.float32)
    input_gate = jax.nn.sigmoid(gates[:, :channels] + gate_bias_ref[0:1, :])
    recur_gate = jax.nn.sigmoid(gates[:, channels:] + gate_bias_ref[1:2, :])
    param = decay_ref[...]
    softplus = jnp.maximum(param, 0.0) + jnp.log1p(jnp.exp(-jnp.abs(param)))
    log_decay = -8.0 * softplus * recur_gate
    decay = jnp.exp(log_decay)
    lost = -jnp.tanh(log_decay) * (decay * decay + 1.0)
    driven = jnp.sqrt(lost) * input_gate * conv_out.astype(jnp.float32)
    parts = channels // LANES
    for j in range(parts):
        a_ref[j] = decay[:, j * LANES : (j + 1) * LANES]
        b_ref[j] = driven[:, j * LANES : (j + 1) * LANES]

    lanes = 8
    length = rows // lanes

    def body(i, carry):
        at = pl.ds(i, lanes, stride=length)
        after = []
        for j in range(parts):
            product, state = carry[j]
            decay_now = a_ref[j, at, :]
            product = product * decay_now
            state = decay_now * state + b_ref[j, at, :]
            a_ref[j, at, :] = product
            b_ref[j, at, :] = state
            after.append((product, state))
        return tuple(after)

    fresh = (jnp.ones((lanes, LANES), jnp.float32), jnp.zeros((lanes, LANES), jnp.float32))
    totals = lax.fori_loop(0, length, body, (fresh,) * parts, unroll=8)
    for j in range(parts):
        product, state = totals[j]
        cols = slice(j * LANES, (j + 1) * LANES)
        start = jnp.zeros((1, LANES), jnp.float32)
        prefix = jnp.ones((1, LANES), jnp.float32)
        for i in range(lanes):
            at = pl.ds(i * length, length)
            within = a_ref[j, at, :]
            state_ref[at, cols] = b_ref[j, at, :] + within * start
            cumulative_ref[at, cols] = within * prefix
            start = product[i : i + 1, :] * start + state[i : i + 1, :]
            prefix = prefix * product[i : i + 1, :]
        end_ref[0:1, cols] = prefix
        end_ref[1:2, cols] = start


def local_scan(rec, before, conv_weight, conv_bias, table, gate_bias, decay_param):
    rows, inner = rec.shape
    width = table.shape[1] // 2
    lead = before.shape[0]

    def columns(height):
        return pl.BlockSpec((height, width), lambda h: (0, h))

    return pl.pallas_call(
        scan_kernel,
        grid=(inner // width,),
        out_shape=(
            jax.ShapeDtypeStruct((rows, inner), jnp.float32),
            jax.ShapeDtypeStruct((rows, inner), jnp.float32),
            jax.ShapeDtypeStruct((2, inner), jnp.float32),
        ),
        in_specs=[
            columns(rows), columns(lead), columns(conv_weight.shape[0]), columns(1),
            pl.BlockSpec((width, 2 * width), lambda h: (h, 0)), columns(2), columns(1),
        ],
        out_specs=(columns(rows), columns(rows), columns(2)),
        scratch_shapes=[
            pltpu.VMEM((rows + lead, width), jnp.float32),
            pltpu.VMEM((width // LANES, rows, LANES), jnp.float32),
            pltpu.VMEM((width // LANES, rows, LANES), jnp.float32),
        ],
    )(
        rec, before, conv_weight, conv_bias.reshape(1, inner), table, gate_bias,
        decay_param.reshape(1, inner),
    )


def shards(
    nz, paired, tokens, norm_gain, lru_proj, gelu_proj, conv_weight, conv_bias, gate_weights,
    gate_bias, decay_param,
):
    seq_count, tok_rows, width = tokens.shape
    inner = lru_proj.shape[1]
    taps = conv_weight.shape[0]
    if paired:
        rec, act, table = gathered_products(
            nz, tokens.reshape(tok_rows, width), norm_gain, lru_proj, gelu_proj, gate_weights
        )
    else:
        flat = tokens.reshape(tok_rows, width).astype(jnp.float32)
        mean_square = jnp.mean(flat * flat, axis=-1, keepdims=True)
        normed = (flat * lax.rsqrt(mean_square + 1e-06) * norm_gain).astype(jnp.bfloat16)
        every = [
            lax.all_gather(w, ("fsdp", "seq"), axis=0, tiled=True) for w in (lru_proj, gelu_proj)
        ]
        rec = jnp.dot(normed, every[0], preferred_element_type=jnp.float32).astype(jnp.bfloat16)
        act = jnp.dot(normed, every[1], preferred_element_type=jnp.float32)
        table = lax.all_gather(gate_weights, "seq", axis=0, tiled=True)
    lead = 8
    before = lax.ppermute(
        rec[tok_rows - lead :, :], "seq", [(i, i + 1) for i in range(nz - 1)]
    )
    local, cumulative, ends = local_scan(
        rec, before, conv_weight, conv_bias, table, gate_bias, decay_param
    )
    every_end = lax.all_gather(ends, "seq")
    position = lax.axis_index("seq")
    start = jnp.zeros((inner,), jnp.float32)
    for k in range(nz - 1):
        start = jnp.where(k < position, every_end[k, 0] * start + every_end[k, 1], start)
    gelu = jax.nn.gelu(act, approximate=True)
    out = ((local + cumulative * start) * gelu).astype(jnp.bfloat16)
    return out.reshape(seq_count, tok_rows, inner)


def solution(mesh):
    placed = (
        P("fsdp", "seq", None), P(), P(("fsdp", "seq"), None), P(("fsdp", "seq"), None), P(), P(),
        P("seq", None), P(), P(),
    )
    nz = mesh.shape["seq"]
    paired = mesh.shape["fsdp"] == 8
    return jax.shard_map(
        functools.partial(shards, nz, paired), mesh=mesh, in_specs=placed,
        out_specs=P("fsdp", "seq", None), check_vma=False,
    )
```

time: 352 us -> 214 us (0.61); the launches traced: 347 us -> 213 us
  Pallas kernels: 0 us -> 188 us
  waiting for transfers between devices: 143 us -> 1.57 us
  other arithmetic: 90 us -> 6.55 us
  local copies, waits for them, and re-layouts: 49.5 us -> 1.38 us
  matrix products: 36.6 us -> 0 us
  blocking collectives: 0 us -> 14.5 us
  between operations: 13.8 us -> 0.04 us
  starting transfers between devices: 13.5 us -> 1.28 us
    pallas_call x0 -> x2, Pallas kernels: none -> 188 us  [the longest x1 169 us: gathered_products(): pl.pallas_call(functools.partial(gather_kernel, nz), out_shape=(jax.Shape...]
    all_gather x3 -> x0, waiting for transfers between devices: 139 us -> none  [the longest x1 115 us: shards(): lax.all_gather(lru_proj, ('fsdp', 'seq'), axis=0, tiled=True)]
    unnamed x66 -> x0, other arithmetic: 57.4 us -> none
    dot_general x3 -> x0, matrix products: 36.6 us -> none  [the longest x1 19.4 us: shards(): jnp.dot(normed, lax.all_gather(gelu_proj, ('fsdp', 'seq'), axis=0, tiled=...]
    reshape x3 -> x0, local copies, waits for them, and re-layouts: 15.7 us -> none  [the longest x2 10.3 us: shards(): gate_all[:, :, block_width:].reshape(seq_count, tok_rows, inner)]
    mul x8 -> x0, other arithmetic: 15.4 us -> none  [the longest x6 11.1 us: block_scan(): running_decay = running_decay * decay_now]
    another operation x1 -> x0, local copies, waits for them, and re-layouts: 15.1 us -> none  [block_scan(): within_decay = jnp.stack(decay_list, axis=2)]
    all_gather x0 -> x1, blocking collectives: none -> 14.5 us  [shards(): every_end = lax.all_gather(ends, 'seq')]
  transfers between devices with their start and end apart: 7 -> 1, of which waited for: 4 -> 1; matrix products, arithmetic and copies ran while one was open for 45% -> 0% of each run, Pallas kernels for 0% -> 0%
where the time goes in v1:
time: 214 us; the launch traced here: 213 us
  Pallas kernels  188 us (88%)
  blocking collectives  14.5 us (7%)
  other arithmetic  6.55 us (3%)
    pallas_call x1, Pallas kernels, gathered_products(): pl.pallas_call(functools.partial(gather_kernel, nz), out_shape=(jax.Shape...  169 us
    pallas_call x1, Pallas kernels, local_scan(): pl.pallas_call(scan_kernel, grid=(inner // width,), out_shape=(jax.ShapeD...  19.5 us
    all_gather x1, blocking collectives, shards(): every_end = lax.all_gather(ends, 'seq')  14.5 us
    reshape x1, other arithmetic, shards(): return out.reshape(seq_count, tok_rows, inner)  6.51 us
  transfers between devices with their start and end apart: 1, of which 1 were waited for; matrix products, arithmetic and copies ran while one was open for 0% of the time, Pallas kernels for 0%

profile of v1, /device:TPU:0, one launch (start us, length us, event | category | flops | bytes accessed | tf_op | source)
XLA Modules:
  0.0 213.5 jit_solution(11136828334225167270)
XLA Ops:
  0.0 168.7 %shard_map.91 = (bf16[512,2048]{1,0:T(8,128)(2,1)}, f32[512,2048]{1,0:T(8,128)}, bf16[2048,512]{1,0:T(8,128)(2,1)}) custom-call(bf16[512,4096]{1,0:T(8,128)(2,1)} %bitcast.12, f32[1,4096]{1,0:T(1,128)} %bitcast.18, bf16[128,2048]{1,0:T(8,128)(2,1)} %lru_ref.1, bf16[128,2048]{1,0:T(8,128)(2,1)} %gelu_ref.1, bf16[512,512]{1,0:T(8,128)(2,1)} %gate_ref.1), custom_call_target="tpu_custom_call" | custom-call | tf_op jit(solution)/shard_map/pallas_call | solution.py:229
  168.7 0.8 slice.21
  169.4 1.3 collective-permute-start
  170.7 1.6 collective-permute-done.before_ref
  172.3 0.0 copy-start
  172.3 0.6 copy-done
  172.9 19.5 %shard_map.92 = (f32[512,2048]{1,0:T(8,128)}, f32[512,2048]{1,0:T(8,128)}, f32[2,2048]{1,0:T(2,128)}) custom-call(bf16[512,2048]{1,0:T(8,128)(2,1)} %get-tuple-element.11.rec_ref, bf16[8,2048]{1,0:T(8,128)(2,1)} %copy-done, f32[4,2048]{1,0:T(4,128)} %weight_ref.1, f32[1,2048]{1,0:T(1,128)} %bitcast.20, bf16[2048,512]{1,0:T(8,128)(2,1)} %get-tuple-element.12.table_ref, ...), custom_call_target="tpu_custom_call" | custom-call | tf_op jit(solution)/shard_map/pallas_call | solution.py:320
  192.4 14.5 %all-gather.1 = f32[4,2,2048]{2,1,0:T(2,128)S(1)} all-gather(f32[1,2,2048]{2,1,0:T(2,128)} %bitcast.19), channel_id=2, replica_groups=mesh['fsdp'=8,'seq'=4] {'seq'}, dimensions={0}, use_global_device_ids=true | all-gather | bytes 81920 | tf_op jit(solution)/shard_map/all_gather | solution.py:372
  207.0 6.5 %fusion.9 = bf16[1,512,2048]{2,1,0:T(8,128)(2,1)} fusion(f32[512,2048]{1,0:T(8,128)} %get-tuple-element.16, f32[512,2048]{1,0:T(8,128)} %get-tuple-element.13, f32[512,2048]{1,0:T(8,128)} %get-tuple-element.14, f32[2048]{0:T(1024)S(1)} %add_select_fusion), kind=kLoop, calls=%fused_computation.10 | loop fusion | flops 12582912 | bytes 14688256 | tf_op jit(solution)/shard_map/reshape | solution.py:379
  (2 shorter events, 0.0 us)
Async XLA Ops:
  169.4 2.9 %collective-permute-start = (bf16[8,2048]{1,0:T(8,128)(2,1)S(1)}, bf16[8,2048]{1,0:T(8,128)(2,1)S(1)}, u32[]{:S(2)}, u32[]{:S(2)}) collective-permute-start(bf16[8,2048]{1,0:T(8,128)(2,1)S(1)} %slice.21), channel_id=1, source_target_pairs={{0,1},{1,2},{2,3},{4,5},{5,6},{6,7},{8,9},{9,10},{10,11},{12,13},{... | collective-permute-start | bytes 98312 | tf_op jit(solution)/shard_map/ppermute | solution.py:366
  172.3 0.6 copy-start

commit v2 on v1

--- a/solution.py
+++ b/solution.py
@@ -25,12 +25,16 @@
     lax.fori_loop(0, tokens_ref.shape[0] // rows, body, 0)
 
 
-def gather_kernel(
+def branch_kernel(
     nz,
     tokens_ref, gain_ref, lru_ref, gelu_ref, gate_ref,
-    rec_ref, act_ref, table_ref,
-    w_ref, normed_ref, own_sem, send_sem, core_send, gate_send,
-    z_recv, gate_recv, x_recv, y_recv, a_recv, b_recv, core_recv,
+    weight_ref, bias_ref, gate_bias_ref, decay_ref,
+    out_ref,
+    w_ref, normed_ref, rec_ref, table_ref, before_ref, padded_ref, a_ref, b_ref,
+    end_ref, carry_ref, start_ref,
+    own_sem, send_sem, core_send, gate_send, gate_core_send, tail_send, carry_send,
+    z_recv, gate_recv, gate_core_recv, x_recv, y_recv, a_recv, b_recv, core_recv,
+    tail_recv, carry_recv,
 ):
     f = lax.axis_index("fsdp")
     z = lax.axis_index("seq")
@@ -43,7 +47,14 @@
     chunks = w_ref.shape[0]
     split = chunks // 2
     gate_rows = gate_ref.shape[0]
-    piece = gate_rows // split
+    gate_steps = split // 2
+    piece = gate_rows // 2 // gate_steps
+    rows = normed_ref.shape[0]
+    channels = table_ref.shape[1] // 2
+    heads = rec_ref.shape[1] // channels
+    pieces = channels // LANES
+    taps = weight_ref.shape[0]
+    lead = before_ref.shape[0]
 
     def remote(src, send, recv, device):
         return pltpu.make_async_remote_copy(
@@ -85,20 +96,20 @@
         return w_ref.at[t, at]
 
     def gate_of(t, source):
-        at = pl.ds(pl.multiple_of(source * gate_rows + t * piece, piece), piece)
-        return table_ref.at[at]
+        first = source * gate_rows + c * (gate_rows // 2) + t * piece
+        return table_ref.at[pl.ds(pl.multiple_of(first, piece), piece)]
 
     def pass_on(t, source, target):
         remote(shard_of(t, source), send_sem.at[t], z_recv.at[t, source], (f, target)).start()
 
-        @pl.when(t < split)
+        @pl.when(t < gate_steps)
         def _():
             remote(gate_of(t, source), gate_send.at[t], gate_recv.at[t, source], (f, target)).start()
 
     def arrived(t, source):
         remote(shard_of(t, source), send_sem.at[t], z_recv.at[t, source], (f, z)).wait_recv()
 
-        @pl.when(t < split)
+        @pl.when(t < gate_steps)
         def _():
             remote(gate_of(t, source), gate_send.at[t], gate_recv.at[t, source], (f, z)).wait_recv()
 
@@ -139,6 +150,21 @@
         remote(mine, send_sem.at[t], x_recv.at[t], (fx, z)).start()
         remote(mine, send_sem.at[t], y_recv.at[t], (fy, z)).start()
         to_core(t, f, 0, line)
+
+        @pl.when(t < gate_steps)
+        def _():
+            for source in range(nz):
+                @pl.when(z != source)
+                def _():
+                    remote(
+                        gate_of(t, source), gate_core_send.at[t], gate_core_recv.at[t], (fc, z)
+                    ).start()
+
+    def gate_done(t):
+        @pl.when(t < gate_steps)
+        def _():
+            others = table_ref.at[pl.ds(0, (nz - 1) * piece)]
+            pltpu.make_async_copy(others, others, gate_core_recv.at[t]).wait()
 
     def sides_done(t):
         from_x = rows_of(fx, t, 0, line)
@@ -172,28 +198,149 @@
 
             @pl.when(t >= split)
             def _():
-                act_ref[at, column] = product
+                chunk = jnp.maximum(t - split, 0)
+                state = b_ref[chunk, at, :] + a_ref[chunk, at, :] * start_ref[0:1, column]
+                out_ref[at, column] = (state * jax.nn.gelu(product, approximate=True)).astype(out_ref.dtype)
 
             return 0
 
         lax.fori_loop(0, blocks, body, 0)
+
+    def columns(h):
+        return pl.ds(pl.multiple_of(h * channels, channels), channels)
+
+    def tail_copy(h, source_rows, device):
+        return pltpu.make_async_remote_copy(
+            src_ref=rec_ref.at[pl.ds(source_rows, lead), columns(h)],
+            dst_ref=before_ref.at[:, columns(h)],
+            send_sem=tail_send.at[h], recv_sem=tail_recv.at[h],
+            device_id=device, device_id_type=MESH,
+        )
+
+    def carry_copy(h, device):
+        return pltpu.make_async_remote_copy(
+            src_ref=carry_ref.at[:, columns(h)], dst_ref=start_ref.at[:, columns(h)],
+            send_sem=carry_send.at[h], recv_sem=carry_recv.at[h],
+            device_id=device, device_id_type=MESH,
+        )
+
+    def send_tail(h):
+        @pl.when(z < nz - 1)
+        def _():
+            tail_copy(h, rows - lead, (f, z + 1)).start()
+
+    def scan(h):
+        @pl.when(z > 0)
+        def _():
+            tail_copy(h, rows - lead, (f, z)).wait_recv()
+
+        cols = columns(h)
+        padded_ref[pl.ds(0, lead), :] = before_ref[:, cols].astype(jnp.float32)
+        padded_ref[pl.ds(lead, rows), :] = rec_ref[:, cols].astype(jnp.float32)
+        conv_sum = jnp.zeros((rows, channels), jnp.float32) + bias_ref[:, cols]
+        for tap in range(taps):
+            conv_sum = conv_sum + weight_ref[tap : tap + 1, cols] * padded_ref[pl.ds(lead - tap, rows), :]
+        conv_out = conv_sum.astype(jnp.bfloat16)
+        gates = jnp.dot(conv_out, table_ref[cols, :], preferred_element_type=jnp.float32)
+        input_gate = jax.nn.sigmoid(gates[:, :channels] + gate_bias_ref[0:1, cols])
+        recur_gate = jax.nn.sigmoid(gates[:, channels:] + gate_bias_ref[1:2, cols])
+        param = decay_ref[:, cols]
+        softplus = jnp.maximum(param, 0.0) + jnp.log1p(jnp.exp(-jnp.abs(param)))
+        log_decay = -8.0 * softplus * recur_gate
+        decay = jnp.exp(log_decay)
+        lost = -jnp.tanh(log_decay) * (decay * decay + 1.0)
+        driven = jnp.sqrt(lost) * input_gate * conv_out.astype(jnp.float32)
+        for j in range(pieces):
+            a_ref[h * pieces + j] = decay[:, j * LANES : (j + 1) * LANES]
+            b_ref[h * pieces + j] = driven[:, j * LANES : (j + 1) * LANES]
+
+        lanes = 8
+        length = rows // lanes
+
+        def body(i, carry):
+            at = pl.ds(i, lanes, stride=length)
+            after = []
+            for j in range(pieces):
+                product, state = carry[j]
+                decay_now = a_ref[h * pieces + j, at, :]
+                product = product * decay_now
+                state = decay_now * state + b_ref[h * pieces + j, at, :]
+                a_ref[h * pieces + j, at, :] = product
+                b_ref[h * pieces + j, at, :] = state
+                after.append((product, state))
+            return tuple(after)
+
+        fresh = (jnp.ones((lanes, LANES), jnp.float32), jnp.zeros((lanes, LANES), jnp.float32))
+        totals = lax.fori_loop(0, length, body, (fresh,) * pieces, unroll=8)
+        for j in range(pieces):
+            product, state = totals[j]
+            start = jnp.zeros((1, LANES), jnp.float32)
+            prefix = jnp.ones((1, LANES), jnp.float32)
+            for i in range(lanes):
+                at = pl.ds(i * length, length)
+                within = a_ref[h * pieces + j, at, :]
+                b_ref[h * pieces + j, at, :] = b_ref[h * pieces + j, at, :] + within * start
+                a_ref[h * pieces + j, at, :] = within * prefix
+                start = product[i : i + 1, :] * start + state[i : i + 1, :]
+                prefix = prefix * product[i : i + 1, :]
+            col = pl.ds(pl.multiple_of((h * pieces + j) * LANES, LANES), LANES)
+            end_ref[0:1, col] = prefix
+            end_ref[1:2, col] = start
+
+    def make_carry(h):
+        cols = columns(h)
+
+        @pl.when(z > 0)
+        def _():
+            carry_copy(h, (f, z)).wait_recv()
+
+        @pl.when(z < nz - 1)
+        def _():
+            end = end_ref[0:1, cols] * start_ref[0:1, cols] + end_ref[1:2, cols]
+            carry_ref[:, cols] = jnp.broadcast_to(end, (carry_ref.shape[0], channels))
+
+    def send_carry(h):
+        @pl.when(z < nz - 1)
+        def _():
+            carry_copy(h, (f, z + 1)).start()
+
+    @pl.when(z == 0)
+    def _():
+        before_ref[...] = jnp.zeros_like(before_ref)
+        start_ref[...] = jnp.zeros_like(start_ref)
 
     stages = [z_first]
     for distance in range(1, nz):
         stages.append(functools.partial(z_hop, distance=distance))
-    stages += [line_done, sides_done, corner_done, multiply]
-    lags = list(range(nz)) + [nz - 1, nz, nz + 1, nz + 2]
-
-    def step(t, _):
-        for stage, lag in zip(stages, lags):
-            @pl.when((t >= lag) & (t < chunks + lag))
+    stages += [line_done, sides_done, corner_done, gate_done, multiply]
+    lags = list(range(nz)) + [nz - 1, nz, nz + 1, nz + 1, nz + 2]
+    scan_at = gate_steps + nz
+
+    def on_head(s, first, stage):
+        @pl.when((s >= first) & (s < first + pieces * heads) & ((s - first) % pieces == 0))
+        def _():
+            stage((s - first) // pieces)
+
+    def step(s, _):
+        for stage, lag in zip(stages[:-1], lags[:-1]):
+            @pl.when((s >= lag) & (s < chunks + lag))
             def _():
-                stage(t - lag)
-
-        @pl.when(t == 0)
+                stage(s - lag)
+
+        on_head(s, scan_at + 2 + 2 * z, send_carry)
+        on_head(s, nz + 2 + pieces, send_tail)
+
+        @pl.when(s == 0)
         def _():
             normalise(tokens_ref, gain_ref, normed_ref)
 
+        on_head(s, scan_at + 1 + 2 * z, make_carry)
+
+        @pl.when((s >= lags[-1]) & (s < chunks + lags[-1]))
+        def _():
+            multiply(s - lags[-1])
+
+        on_head(s, scan_at, scan)
         return 0
 
     lax.fori_loop(0, chunks + lags[-1], step, 0)
@@ -207,45 +354,71 @@
                 sent = w_ref.at[t, pl.ds(0, shards_sent * shard + 3 * line)]
                 pltpu.make_async_copy(sent, sent, send_sem.at[t]).wait()
 
-                @pl.when(t < split)
+                @pl.when(t < gate_steps)
                 def _():
                     sent_gate = table_ref.at[pl.ds(0, shards_sent * piece)]
                     pltpu.make_async_copy(sent_gate, sent_gate, gate_send.at[t]).wait()
 
         whole = w_ref.at[t, pl.ds(0, 4 * line)]
         pltpu.make_async_copy(whole, whole, core_send.at[t]).wait()
+
+        @pl.when(t < gate_steps)
+        def _():
+            others = table_ref.at[pl.ds(0, (nz - 1) * piece)]
+            pltpu.make_async_copy(others, others, gate_core_send.at[t]).wait()
+
+        @pl.when((t < heads) & (z < nz - 1))
+        def _():
+            tail_copy(t, rows - lead, (f, z)).wait_send()
+            carry_copy(t, (f, z)).wait_send()
+
         return 0
 
     lax.fori_loop(0, chunks, drain, 0)
 
 
-def gathered_products(nz, tokens, norm_gain, lru_proj, gelu_proj, gate_weights):
+def fused_branch(
+    nz, tokens, norm_gain, lru_proj, gelu_proj, conv_weight, conv_bias, gate_weights, gate_bias,
+    decay_param,
+):
     rows, width = tokens.shape
     inner = lru_proj.shape[1]
     chunks = 2 * inner // LANES
+    channels = gate_weights.shape[1] // 2
+    heads = inner // channels
     vmem = pl.BlockSpec(memory_space=pltpu.VMEM)
     any_ = pl.BlockSpec(memory_space=pl.ANY)
     dma = pltpu.SemaphoreType.DMA
+    f32, bf16 = jnp.float32, jnp.bfloat16
+    lead = 16
     return pl.pallas_call(
-        functools.partial(gather_kernel, nz),
-        out_shape=(
-            jax.ShapeDtypeStruct((rows, inner), jnp.bfloat16),
-            jax.ShapeDtypeStruct((rows, inner), jnp.float32),
-            jax.ShapeDtypeStruct((gate_weights.shape[0] * nz, gate_weights.shape[1]), jnp.bfloat16),
-        ),
-        in_specs=[vmem, vmem, any_, any_, any_],
-        out_specs=(vmem, vmem, vmem),
+        functools.partial(branch_kernel, nz),
+        out_shape=jax.ShapeDtypeStruct((rows, inner), bf16),
+        in_specs=[vmem, vmem, any_, any_, any_, vmem, vmem, vmem, vmem],
+        out_specs=vmem,
         scratch_shapes=[
-            pltpu.VMEM((chunks, width, LANES), jnp.bfloat16),
-            pltpu.VMEM((rows, width), jnp.bfloat16),
-            dma((2,)), dma((chunks,)), dma((chunks,)), dma((chunks // 2,)),
-            dma((chunks, nz)), dma((chunks // 2, nz)),
+            pltpu.VMEM((chunks, width, LANES), bf16),
+            pltpu.VMEM((rows, width), bf16),
+            pltpu.VMEM((rows, inner), bf16),
+            pltpu.VMEM((gate_weights.shape[0] * nz, 2 * channels), bf16),
+            pltpu.VMEM((lead, inner), bf16),
+            pltpu.VMEM((lead + rows, channels), f32),
+            pltpu.VMEM((chunks // 2, rows, LANES), f32),
+            pltpu.VMEM((chunks // 2, rows, LANES), f32),
+            pltpu.VMEM((8, inner), f32), pltpu.VMEM((8, inner), f32), pltpu.VMEM((8, inner), f32),
+            dma((2,)), dma((chunks,)), dma((chunks,)), dma((chunks // 4,)), dma((chunks // 4,)),
+            dma((heads,)), dma((heads,)),
+            dma((chunks, nz)), dma((chunks // 4, nz)), dma((chunks // 4,)),
             dma((chunks,)), dma((chunks,)), dma((chunks,)), dma((chunks,)), dma((chunks,)),
+            dma((heads,)), dma((heads,)),
         ],
         compiler_params=pltpu.CompilerParams(
             collective_id=0, has_side_effects=True, vmem_limit_bytes=VMEM_BYTES
         ),
-    )(tokens, norm_gain.reshape(1, width), lru_proj, gelu_proj, gate_weights)
+    )(
+        tokens, norm_gain.reshape(1, width), lru_proj, gelu_proj, gate_weights, conv_weight,
+        conv_bias.reshape(1, inner), gate_bias, decay_param.reshape(1, inner),
+    )
 
 
 def scan_kernel(
@@ -349,19 +522,20 @@
     inner = lru_proj.shape[1]
     taps = conv_weight.shape[0]
     if paired:
-        rec, act, table = gathered_products(
-            nz, tokens.reshape(tok_rows, width), norm_gain, lru_proj, gelu_proj, gate_weights
+        out = fused_branch(
+            nz, tokens.reshape(tok_rows, width), norm_gain, lru_proj, gelu_proj, conv_weight,
+            conv_bias, gate_weights, gate_bias, decay_param,
         )
-    else:
-        flat = tokens.reshape(tok_rows, width).astype(jnp.float32)
-        mean_square = jnp.mean(flat * flat, axis=-1, keepdims=True)
-        normed = (flat * lax.rsqrt(mean_square + 1e-06) * norm_gain).astype(jnp.bfloat16)
-        every = [
-            lax.all_gather(w, ("fsdp", "seq"), axis=0, tiled=True) for w in (lru_proj, gelu_proj)
-        ]
-        rec = jnp.dot(normed, every[0], preferred_element_type=jnp.float32).astype(jnp.bfloat16)
-        act = jnp.dot(normed, every[1], preferred_element_type=jnp.float32)
-        table = lax.all_gather(gate_weights, "seq", axis=0, tiled=True)
+        return out.reshape(seq_count, tok_rows, inner)
+    flat = tokens.reshape(tok_rows, width).astype(jnp.float32)
+    mean_square = jnp.mean(flat * flat, axis=-1, keepdims=True)
+    normed = (flat * lax.rsqrt(mean_square + 1e-06) * norm_gain).astype(jnp.bfloat16)
+    every = [
+        lax.all_gather(w, ("fsdp", "seq"), axis=0, tiled=True) for w in (lru_proj, gelu_proj)
+    ]
+    rec = jnp.dot(normed, every[0], preferred_element_type=jnp.float32).astype(jnp.bfloat16)
+    act = jnp.dot(normed, every[1], preferred_element_type=jnp.float32)
+    table = lax.all_gather(gate_weights, "seq", axis=0, tiled=True)
     lead = 8
     before = lax.ppermute(
         rec[tok_rows - lead :, :], "seq", [(i, i + 1) for i in range(nz - 1)]
@@ -385,7 +559,7 @@
         P("seq", None), P(), P(),
     )
     nz = mesh.shape["seq"]
-    paired = mesh.shape["fsdp"] == 8
+    paired = mesh.shape["fsdp"] == 8 and 1 < nz <= 5
     return jax.shard_map(
         functools.partial(shards, nz, paired), mesh=mesh, in_specs=placed,
         out_specs=P("fsdp", "seq", None), check_vma=False,

time: 214 us -> 176 us (0.82)
  Pallas kernels: 188 us -> 172 us
  blocking collectives: 14.5 us -> 0 us
  other arithmetic: 6.55 us -> 0 us
    pallas_call x2 -> x1, Pallas kernels: 188 us -> 172 us  [fused_branch(): pl.pallas_call(functools.partial(branch_kernel, nz), out_shape=jax.ShapeD...]
    all_gather x1 -> x0, blocking collectives: 14.5 us -> none  [shards(): every_end = lax.all_gather(ends, 'seq')]
    reshape x1 -> x0, other arithmetic: 6.51 us -> none  [shards(): return out.reshape(seq_count, tok_rows, inner)]
    unnamed x2 -> x1, local copies, waits for them, and re-layouts: 0.61 us -> 3.16 us
  transfers between devices with their start and end apart: 1 -> 0, of which waited for: 1 -> 0; matrix products, arithmetic and copies ran while one was open for 0% -> 0% of each run, Pallas kernels for 0% -> 0%
where the time goes in v2:
time: 176 us
  Pallas kernels  172 us (98%)
  local copies, waits for them, and re-layouts  3.16 us (2%)
    pallas_call x1, Pallas kernels, fused_branch(): pl.pallas_call(functools.partial(branch_kernel, nz), out_shape=jax.ShapeD...  172 us

profile of v2, /device:TPU:0, one launch (start us, length us, event | category | flops | bytes accessed | tf_op | source)
XLA Modules:
  0.0 175.7 jit_solution(6249464790262119424)
XLA Ops:
  0.0 172.5 %shard_map.91 = bf16[512,2048]{1,0:T(8,128)(2,1)} custom-call(bf16[512,4096]{1,0:T(8,128)(2,1)} %bitcast.6, f32[1,4096]{1,0:T(1,128)} %bitcast.7, bf16[128,2048]{1,0:T(8,128)(2,1)} %lru_ref.1, bf16[128,2048]{1,0:T(8,128)(2,1)} %gelu_ref.1, bf16[512,512]{1,0:T(8,128)(2,1)} %gate_ref.1, f32[4,2048]{1,0:T(4,128)} %weight_ref.1, f32[1,2048]{1,0:T(1,128)} %bitcast.8, ...), custom_call_target="tpu_custom_call" | custom-call | tf_op jit(solution)/shard_map/pallas_call | solution.py:394
  172.5 3.2 %copy.11 = bf16[1,512,2048]{2,1,0:T(8,128)(2,1)} copy(bf16[1,512,2048]{2,1,0:T(8,128)(2,1)} %bitcast.5) | data formatting | bytes 4194304

commit v3 on v2

--- a/solution.py
+++ b/solution.py
@@ -313,7 +313,7 @@
     for distance in range(1, nz):
         stages.append(functools.partial(z_hop, distance=distance))
     stages += [line_done, sides_done, corner_done, gate_done, multiply]
-    lags = list(range(nz)) + [nz - 1, nz, nz + 1, nz + 1, nz + 2]
+    lags = list(range(nz)) + [nz - 1, nz + 1, nz + 2, nz + 1, nz + 3]
     scan_at = gate_steps + nz
 
     def on_head(s, first, stage):
@@ -328,7 +328,7 @@
                 stage(s - lag)
 
         on_head(s, scan_at + 2 + 2 * z, send_carry)
-        on_head(s, nz + 2 + pieces, send_tail)
+        on_head(s, lags[-1] + pieces, send_tail)
 
         @pl.when(s == 0)
         def _():

time: 176 us -> 178 us (1.011)
  Pallas kernels: 172 us -> 175 us
    pallas_call x1, Pallas kernels: 172 us -> 175 us  [fused_branch(): pl.pallas_call(functools.partial(branch_kernel, nz), out_shape=jax.ShapeD...]
where the time goes in v3:
time: 178 us
  Pallas kernels  175 us (98%)
  local copies, waits for them, and re-layouts  3.16 us (2%)
    pallas_call x1, Pallas kernels, fused_branch(): pl.pallas_call(functools.partial(branch_kernel, nz), out_shape=jax.ShapeD...  175 us

profile of v3, /device:TPU:0, one launch (start us, length us, event | category | flops | bytes accessed | tf_op | source)
XLA Modules:
  0.0 177.9 jit_solution(6910542141021545869)
XLA Ops:
  0.0 174.8 %shard_map.91 = bf16[512,2048]{1,0:T(8,128)(2,1)} custom-call(bf16[512,4096]{1,0:T(8,128)(2,1)} %bitcast.6, f32[1,4096]{1,0:T(1,128)} %bitcast.7, bf16[128,2048]{1,0:T(8,128)(2,1)} %lru_ref.1, bf16[128,2048]{1,0:T(8,128)(2,1)} %gelu_ref.1, bf16[512,512]{1,0:T(8,128)(2,1)} %gate_ref.1, f32[4,2048]{1,0:T(4,128)} %weight_ref.1, f32[1,2048]{1,0:T(1,128)} %bitcast.8, ...), custom_call_target="tpu_custom_call" | custom-call | tf_op jit(solution)/shard_map/pallas_call | solution.py:394
  174.8 3.2 %copy.11 = bf16[1,512,2048]{2,1,0:T(8,128)(2,1)} copy(bf16[1,512,2048]{2,1,0:T(8,128)(2,1)} %bitcast.5) | data formatting | bytes 4194304

commit v4 on v2

--- a/solution.py
+++ b/solution.py
@@ -12,7 +12,7 @@
 VMEM_BYTES = 66_000_000
 
 
-def normalise(tokens_ref, gain_ref, normed_ref):
+def normalise(tokens_ref, gain_ref, normed_ref, part, parts):
     rows = 32
 
     def body(i, _):
@@ -22,7 +22,8 @@
         normed_ref[at, :] = (values * lax.rsqrt(mean_square + 1e-06) * gain_ref[...]).astype(jnp.bfloat16)
         return 0
 
-    lax.fori_loop(0, tokens_ref.shape[0] // rows, body, 0)
+    blocks = tokens_ref.shape[0] // rows // parts
+    lax.fori_loop(part * blocks, (part + 1) * blocks, body, 0)
 
 
 def branch_kernel(
@@ -330,9 +331,9 @@
         on_head(s, scan_at + 2 + 2 * z, send_carry)
         on_head(s, nz + 2 + pieces, send_tail)
 
-        @pl.when(s == 0)
-        def _():
-            normalise(tokens_ref, gain_ref, normed_ref)
+        @pl.when(s < 4)
+        def _():
+            normalise(tokens_ref, gain_ref, normed_ref, s, 4)
 
         on_head(s, scan_at + 1 + 2 * z, make_carry)
 

time: 176 us -> 176 us (level)
  no operation moved by 1% of the time
where the time goes in v4:
time: 176 us; the launch traced here: 175 us
  Pallas kernels  172 us (98%)
  local copies, waits for them, and re-layouts  3.16 us (2%)
    pallas_call x1, Pallas kernels, fused_branch(): pl.pallas_call(functools.partial(branch_kernel, nz), out_shape=jax.ShapeD...  172 us

profile of v4, /device:TPU:0, one launch (start us, length us, event | category | flops | bytes accessed | tf_op | source)
XLA Modules:
  0.0 175.4 jit_solution(14050112072688358914)
XLA Ops:
  0.0 172.2 %shard_map.91 = bf16[512,2048]{1,0:T(8,128)(2,1)} custom-call(bf16[512,4096]{1,0:T(8,128)(2,1)} %bitcast.6, f32[1,4096]{1,0:T(1,128)} %bitcast.7, bf16[128,2048]{1,0:T(8,128)(2,1)} %lru_ref.1, bf16[128,2048]{1,0:T(8,128)(2,1)} %gelu_ref.1, bf16[512,512]{1,0:T(8,128)(2,1)} %gate_ref.1, f32[4,2048]{1,0:T(4,128)} %weight_ref.1, f32[1,2048]{1,0:T(1,128)} %bitcast.8, ...), custom_call_target="tpu_custom_call" | custom-call | tf_op jit(solution)/shard_map/pallas_call | solution.py:395
  172.2 3.2 %copy.11 = bf16[1,512,2048]{2,1,0:T(8,128)(2,1)} copy(bf16[1,512,2048]{2,1,0:T(8,128)(2,1)} %bitcast.5) | data formatting | bytes 4194304

commit v5 on v4

--- a/solution.py
+++ b/solution.py
@@ -186,11 +186,11 @@
     def multiply(t):
         whole = w_ref.at[t, pl.ds(0, 4 * line)]
         pltpu.make_async_copy(whole, whole, core_recv.at[t]).wait()
-        blocks = normed_ref.shape[0] // 256
+        blocks = normed_ref.shape[0] // 512
         column = pl.ds(pl.multiple_of((t % split) * LANES, LANES), LANES)
 
         def body(i, _):
-            at = pl.ds(pl.multiple_of(i * 256, 256), 256)
+            at = pl.ds(pl.multiple_of(i * 512, 512), 512)
             product = jnp.dot(normed_ref[at, :], w_ref[t], preferred_element_type=jnp.float32)
 
             @pl.when(t < split)

time: 176 us -> 174 us (0.989)
  no operation moved by 1% of the time
where the time goes in v5:
time: 174 us
  Pallas kernels  171 us (98%)
  local copies, waits for them, and re-layouts  3.16 us (2%)
    pallas_call x1, Pallas kernels, fused_branch(): pl.pallas_call(functools.partial(branch_kernel, nz), out_shape=jax.ShapeD...  171 us

profile of v5, /device:TPU:0, one launch (start us, length us, event | category | flops | bytes accessed | tf_op | source)
XLA Modules:
  0.0 173.8 jit_solution(15586214968384202992)
XLA Ops:
  0.0 170.6 %shard_map.91 = bf16[512,2048]{1,0:T(8,128)(2,1)} custom-call(bf16[512,4096]{1,0:T(8,128)(2,1)} %bitcast.6, f32[1,4096]{1,0:T(1,128)} %bitcast.7, bf16[128,2048]{1,0:T(8,128)(2,1)} %lru_ref.1, bf16[128,2048]{1,0:T(8,128)(2,1)} %gelu_ref.1, bf16[512,512]{1,0:T(8,128)(2,1)} %gate_ref.1, f32[4,2048]{1,0:T(4,128)} %weight_ref.1, f32[1,2048]{1,0:T(1,128)} %bitcast.8, ...), custom_call_target="tpu_custom_call" | custom-call | tf_op jit(solution)/shard_map/pallas_call | solution.py:395
  170.7 3.2 %copy.11 = bf16[1,512,2048]{2,1,0:T(8,128)(2,1)} copy(bf16[1,512,2048]{2,1,0:T(8,128)(2,1)} %bitcast.5) | data formatting | bytes 4194304
